TPU v7x, 128 devices: a whole 4x4x4 slice. The times are simulated.
128 devices in a mesh: dp: 1, ep: 128 (over z, y, x, core).
Axes of the slice: x: 4, y: 4, z: 4, core: 2. Of those that a mesh axis runs over, the one named last changes fastest.
Arguments:
- tokens: bfloat16 [32768, 2048], P(('dp', 'ep'))
- routes: int32 [32768, 8], P(('dp', 'ep'))
- w_router: bfloat16 [2048, 128], replicated
- w_one: bfloat16 [128, 2048, 768], P('ep')
- w_three: bfloat16 [128, 2048, 768], P('ep')
- w_two: bfloat16 [128, 768, 2048], P('ep')
Outputs:
- output: bfloat16 [32768, 2048], P(('dp', 'ep'))
All inputs are finite; a program needn't handle non-finite values.
Results may differ from a plain program's by a relative error of at most 0.00819171.
Values are sent between devices in bfloat16 or wider.
A program may use at most 1 GiB of HBM per device.

v0:
```python
import functools

import jax
import jax.numpy as jnp
from jax import lax
from jax.experimental import pallas as pl
from jax.experimental.pallas import tpu as pltpu
from jax.sharding import PartitionSpec as P

MESH = pl.DeviceIdType.MESH
Z, Y, X = 0, 1, 2
ORDERS = ((Z, Y, X), (X, Z, Y), (Y, X, Z))
SLOTS = 8


def slot_capacity(num_tokens, top_k, num_experts):
    return 8 * ((3 * num_tokens * top_k + 16 * num_experts - 1) // (16 * num_experts))


def torus_side(group_size):
    side = 1
    while 2 * side ** 3 < group_size:
        side += 1
    return side


def column_groups(d_model):
    lanes = d_model // 128
    count = 6 if lanes >= 6 else 3
    widths = [128 * (lanes // count + (1 if i < lanes % count else 0)) for i in range(count)]
    starts = [sum(widths[:i]) for i in range(count)]
    return list(zip(starts, widths))


def moved(me, side, axis, steps, core_steps=0):
    digits = [me // (2 * side * side), (me // (2 * side)) % side, (me // 2) % side]
    digits[axis] = (digits[axis] + steps + side) % side
    return ((digits[Z] * side + digits[Y]) * side + digits[X]) * 2 + (me + core_steps) % 2


def plane_experts(me, side, order, num_tokens):
    bits = side.bit_length() - 1
    position = lax.broadcasted_iota(jnp.int32, (2 * side * side, num_tokens), 0)
    digits = [me // (2 * side * side), (me // (2 * side)) % side, (me // 2) % side]
    for place, axis in enumerate(order[1:]):
        steps = jnp.right_shift(position, 1 + (1 - place) * bits)
        digits[axis] = jnp.bitwise_and(digits[axis] + steps, side - 1)
    core = jnp.bitwise_and(me + position, 1)
    return ((digits[Z] * side + digits[Y]) * side + digits[X]) * 2 + core


def each(first, end, act):
    def step(i, carry):
        act(i)
        return carry
    lax.fori_loop(first, end, step, 0)


def moe_kernel(side, chunks, groups, tokens_hbm, routes_ref, w_router_hbm, w_one_hbm, w_three_hbm, w_two_hbm, y_own, y_peers,
               toks, infos, own_info, plans, packed, relay, rows, w_router, w_one, w_three, w_two, parts, mids,
               load_sem, w_sem, s0_sem, r0_sem, sp_sem, rp_sem, s1_sem, r1_sem, s2_sem, r2_sem, b1_sem, c1_sem, b2_sem, c2_sem, s3_sem, r3_sem, out_sem, free2_sem, free3_sem):
    me = lax.axis_index('ep')
    dp = lax.axis_index('dp')
    num_tokens = tokens_hbm.shape[0]
    plane = 2 * side * side
    ends = 2 * side
    count = len(groups)
    arrival = (0, 1, 4, 2, 3, 5) if count == 6 else (1, 0, 2)
    near = (1, side - 1) if side > 2 else (1,)
    far = side > 2
    packed_rows = plane * SLOTS
    top_k = routes_ref.shape[0]
    orders = [ORDERS[g % 3] for g in range(count)]

    def remote(src, dst, s_sem, r_sem, axis, steps, core_steps=0):
        return pltpu.make_async_remote_copy(
            src_ref=src, dst_ref=dst, send_sem=s_sem, recv_sem=r_sem,
            device_id=(dp, moved(me, side, axis, steps, core_steps)), device_id_type=MESH)

    def columns(g):
        return pl.ds(*groups[g])

    def relay_from(g, q, b):
        return relay[g].at[q, b] if g % 3 == 1 else relay[g].at[q, :, b]

    def relay_others(g, q):
        return relay[g].at[q, pl.ds(1, side - 1)] if g % 3 == 1 else relay[g].at[q, :, pl.ds(1, side - 1)]

    def rows_at(g, q, e):
        c, core = e // 2, e % 2
        third = orders[g][2]
        where = {Z: (q, c, slice(None), slice(None), core), Y: (q, slice(None), c, slice(None), core),
                 X: (q, slice(None), slice(None), c, core)}[third]
        return where + (slice(None), columns(g))

    def half(i):
        return pl.ds(i * (num_tokens // 2), num_tokens // 2)

    def gather_near(g, d, i):
        part = half(i if d == 0 else 1 - i)
        return remote(toks[g].at[0, part], toks[g].at[near[d], part],
                      s0_sem.at[g, 2 * d + i], r0_sem.at[g, 2 * d + i], orders[g][0], near[d])

    def gather_far(g, d):
        return remote(toks[g].at[near[d], half(d)], toks[g].at[2, half(d)],
                      s0_sem.at[g, 4 + d], r0_sem.at[g, 4 + d], orders[g][0], near[d])

    def gather_info(o, a):
        return remote(own_info, infos.at[o, a], sp_sem.at[o], rp_sem.at[o], ORDERS[o][0], a)

    def gather_info_all(o):
        others = infos.at[o, pl.ds(1, side - 1)]
        return remote(others, others, sp_sem.at[o], rp_sem.at[o], ORDERS[o][0], 1)

    def relay_slab(g, q, a, b):
        return relay[g].at[q, b, a] if g % 3 == 1 else relay[g].at[q, a, b]

    def out_second(g, q, a, b):
        return remote(packed[g].at[q, b, a], relay_slab(g, q, a, b), s1_sem.at[g, q], r1_sem.at[g, q], orders[g][1], b)

    def out_second_all(g, q):
        return remote(packed[g].at[q, pl.ds(1, side - 1)], relay_others(g, q), s1_sem.at[g, q], r1_sem.at[g, q], orders[g][1], 1)

    def out_third(g, q, e):
        return remote(relay[g].at[q, :, :, e], rows.at[rows_at(g, q, e)], s2_sem.at[g, q], r2_sem.at[g, q], orders[g][2], e // 2, e % 2)

    def third_all(g, q, s_sem, r_sem):
        some = relay[g].at[q, :, :, pl.ds(1, ends - 1)]
        return remote(some, some, s_sem.at[g, q], r_sem.at[g, q], orders[g][2], 1)

    def home_third(g, q, e):
        return remote(rows.at[rows_at(g, q, e)], relay[g].at[q, :, :, e], b1_sem.at[g, q], c1_sem.at[g, q], orders[g][2], -(e // 2), e % 2)

    def home_second(g, q, b):
        return remote(relay_from(g, q, b), packed[g].at[q, b], b2_sem.at[g, q], c2_sem.at[g, q], orders[g][1], -b)

    def home_second_all(g, q):
        return remote(relay_others(g, q), packed[g].at[q, pl.ds(1, side - 1)], b2_sem.at[g, q], c2_sem.at[g, q], orders[g][1], 1)

    def home_mid(g, d):
        return remote(parts.at[2, half(d), columns(g)], mids.at[d, :, columns(g)],
                      s3_sem.at[g, d], r3_sem.at[g, d], orders[g][0], -near[d])

    def home_near(g, d, i):
        part = half(1 - d if i == 0 else d)
        return remote(parts.at[near[d], part, columns(g)], y_peers.at[d, part, columns(g)],
                      s3_sem.at[g, 2 + 2 * d + i], r3_sem.at[g, 2 + 2 * d + i], orders[g][0], -near[d])

    def tell(sem, axis, steps, core_steps=0):
        pl.semaphore_signal(sem, inc=1, device_id=(dp, moved(me, side, axis, steps, core_steps)), device_id_type=MESH)

    loads = [pltpu.make_async_copy(tokens_hbm.at[:, columns(g)], toks[g].at[0], load_sem.at[g]) for g in range(count)]
    loads.append(pltpu.make_async_copy(w_router_hbm, w_router, load_sem.at[count]))
    weights = [pltpu.make_async_copy(src, dst, w_sem.at[i]) for i, (src, dst) in enumerate(
        [(w_one_hbm, w_one), (w_three_hbm, w_three), (w_two_hbm, w_two)])]
    barrier = pltpu.get_barrier_semaphore()
    tell(barrier, X, 0, 1)
    for axis in (Z, Y, X):
        for steps in range(1, side):
            for core_steps in range(2):
                tell(barrier, axis, steps, core_steps)
    for copy in loads:
        copy.start()
    with jax.named_scope('own_wait'):
        for copy in loads:
            copy.wait()
    with jax.named_scope('barrier'):
        pl.semaphore_wait(barrier, 1 + 3 * (side - 1) * 2)

    for i in range(2):
        for g in range(count):
            for d in range(len(near)):
                gather_near(g, d, i).start()

    num_experts = 2 * side ** 3
    logits = sum(jnp.dot(toks[g][0], w_router[columns(g), :], preferred_element_type=jnp.float32) for g in range(count)).T
    ids = lax.broadcasted_iota(jnp.int32, (num_experts, num_tokens), 0)
    picks = [routes_ref[k:k + 1, :] for k in range(top_k)]
    scores = [jnp.sum(jnp.where(pick == ids, logits, 0.0), axis=0, keepdims=True) for pick in picks]
    peak = functools.reduce(jnp.maximum, scores)
    scores = [jnp.exp(score - peak) for score in scores]
    norm = sum(scores)
    for k in range(top_k):
        own_info[k:k + 1, :] = picks[k].astype(jnp.float32)
        own_info[top_k + k:top_k + k + 1, :] = scores[k] / norm
    for o in range(3):
        for a in range(1, side):
            gather_info(o, a).start()
    before = (lax.broadcasted_iota(jnp.int32, (num_tokens, num_tokens), 0)
              < lax.broadcasted_iota(jnp.int32, (num_tokens, num_tokens), 1))
    before = jnp.where(before, 1.0, 0.0).astype(jnp.bfloat16)
    expert_at = [plane_experts(me, side, order, num_tokens).astype(jnp.float32) for order in ORDERS]

    def make_plan(o, a, info):
        mask = jnp.zeros((plane, num_tokens), jnp.float32)
        gate = jnp.zeros((plane, num_tokens), jnp.float32)
        for k in range(top_k):
            hit = info[k:k + 1] == expert_at[o]
            mask = jnp.where(hit, 1.0, mask)
            gate = jnp.where(hit, info[top_k + k:top_k + k + 1], gate)
        slot = jnp.dot(mask.astype(jnp.bfloat16), before, preferred_element_type=jnp.float32)
        plans[o][a, pl.ds(0, plane), :] = jnp.where(mask > 0.0, slot, -1.0)
        plans[o][a, pl.ds(plane, plane), :] = gate

    for o in range(3):
        make_plan(o, 0, own_info[...])
    for copy in weights:
        copy.start()

    def taken(g, q, a):
        slots = plans[g % 3][a, pl.ds(0, plane), :]
        ids = lax.broadcasted_iota(jnp.int32, (plane, SLOTS, num_tokens), 1) + q * SLOTS
        return jnp.broadcast_to(slots[:, None, :], (plane, SLOTS, num_tokens)) == ids.astype(jnp.float32)

    def pack(g, q, a):
        select = jnp.where(taken(g, q, a), 1.0, 0.0).reshape(packed_rows, num_tokens).astype(jnp.bfloat16)
        out = jnp.dot(select, toks[g][a], preferred_element_type=jnp.float32)
        out = out.reshape(side, ends, SLOTS, groups[g][1]).astype(jnp.bfloat16)
        packed[g][q, pl.ds(1, side - 1), a] = out[1:]
        each(1, side, lambda b: out_second(g, q, a, b).start())
        relay_slab(g, q, a, 0)[...] = out[0]

    def pack_own(q, carry):
        for g in range(count):
            pack(g, q, 0)
        return carry

    if far:
        with jax.named_scope('gather_far'):
            for g in range(count):
                for d in range(2):
                    gather_near(g, d, 0).wait_recv()
                    gather_far(g, d).start()
    with jax.named_scope('pack_own'):
        lax.fori_loop(0, chunks, pack_own, 0)
    parts[...] = jnp.zeros_like(parts)
    with jax.named_scope('gather_wait'):
        for o in range(3):
            gather_info_all(o).wait_recv()
            for a in range(1, side):
                make_plan(o, a, infos[o, a])
        for g in range(count):
            for d in range(len(near)):
                if not far:
                    gather_near(g, d, 0).wait_recv()
                gather_near(g, d, 1).wait_recv()
            if far:
                gather_far(g, 0).wait_recv()
                gather_far(g, 1).wait_recv()

    def outward(i, carry):
        @pl.when(i < chunks)
        def _():
            for g in range(count):
                def source(a, c):
                    pack(g, i, a)
                    return c
                with jax.named_scope('pack'):
                    lax.fori_loop(1, side, source, 0)

        @pl.when(i > 0)
        def _():
            forward(i - 1)
        return carry

    def forward(q):
        for g in range(count):
            with jax.named_scope('s1_wait'):
                out_second_all(g, q).wait_recv()
            each(1, ends, lambda e: out_third(g, q, e).start())
            rows[rows_at(g, q, 0)] = relay[g][q, :, :, 0]
            with jax.named_scope('s1_send_wait'):
                out_second_all(g, q).wait_send()
            each(1, side, lambda b: tell(free2_sem.at[g, q], orders[g][1], b))

    lax.fori_loop(0, chunks + 1, outward, 0)
    for copy in weights:
        copy.wait()

    def experts(q, carry):
        with jax.named_scope('s2_wait'):
            for g in range(count):
                third_all(g, q, s2_sem, r2_sem).wait_recv()
        for g in range(count):
            with jax.named_scope('s2_send_wait'):
                third_all(g, q, s2_sem, r2_sem).wait_send()
            each(1, ends, lambda e: tell(free3_sem.at[g, q], orders[g][2], e // 2, e % 2))

        def block(z, c):
            shape = rows.shape[2:]
            u = rows[q, z].astype(jnp.float32).reshape(packed_rows, shape[-1]).astype(jnp.bfloat16)
            gate_pre = jnp.dot(u, w_one[...], preferred_element_type=jnp.float32)
            up_pre = jnp.dot(u, w_three[...], preferred_element_type=jnp.float32)
            hidden = (jax.nn.silu(gate_pre) * up_pre).astype(jnp.bfloat16)
            out = jnp.dot(hidden, w_two[...], preferred_element_type=jnp.float32)
            rows[q, z] = out.reshape(shape).astype(jnp.bfloat16)
            return c
        with jax.named_scope('mlp'):
            lax.fori_loop(0, side, block, 0)
        for g in range(count):
            with jax.named_scope('free3'):
                pl.semaphore_wait(free3_sem.at[g, q], ends - 1)
            each(1, ends, lambda e: home_third(g, q, e).start())
            relay[g][q, :, :, 0] = rows[rows_at(g, q, 0)]
        return carry

    lax.fori_loop(0, chunks, experts, 0)

    def backward(q):
        for g in range(count):
            with jax.named_scope('r1_wait'):
                third_all(g, q, b1_sem, c1_sem).wait_recv()
            pl.semaphore_wait(free2_sem.at[g, q], side - 1)
            each(1, side, lambda b: home_second(g, q, b).start())
            packed[g][q, 0] = relay_from(g, q, 0)[...]

    ahead = w_one.shape[1] >= 3 * packed_rows and w_one.shape[0] >= 2 * side * num_tokens

    def gate_rows(o, a):
        return pl.ds(pl.multiple_of(((o % 2) * side + a) * num_tokens, num_tokens), num_tokens)

    def gate_parts(g, q, a):
        gates = plans[g % 3][a, pl.ds(plane, plane), :]
        used = taken(g, q, a)
        for _ in range(3):
            part = gates.astype(jnp.bfloat16).astype(jnp.float32)
            gates = gates - part
            yield jnp.where(used, jnp.broadcast_to(part[:, None, :], used.shape), 0.0).reshape(packed_rows, num_tokens)

    def build_gates(q):
        for o in range(3):
            def build(a):
                for i, mix in enumerate(gate_parts(o, q, a)):
                    home = w_one if o < 2 else w_three
                    home[gate_rows(o, a), i * packed_rows:(i + 1) * packed_rows] = mix.T.astype(jnp.bfloat16)
            each(0, side, build)

    def combine(q):
        last = q == chunks - 1
        if ahead:
            with jax.named_scope('gates_ahead'):
                build_gates(q)
        for g in arrival:
            with jax.named_scope('r2_wait'):
                home_second_all(g, q).wait_recv()
            width = groups[g][1]

            def source(i, c):
                a = (i + side // 2) % side
                o = packed[g][q, :, a].astype(jnp.float32).reshape(packed_rows, width).astype(jnp.bfloat16)
                if ahead:
                    mixes = w_one if g % 3 < 2 else w_three
                    terms = [jnp.dot(mixes[gate_rows(g % 3, a), i * packed_rows:(i + 1) * packed_rows], o, preferred_element_type=jnp.float32)
                             for i in range(3)]
                else:
                    terms = [lax.dot_general(mix.astype(jnp.bfloat16), o, (((0,), (0,)), ((), ())), preferred_element_type=jnp.float32)
                             for mix in gate_parts(g, q, a)]
                parts[a, :, columns(g)] += terms[0] + terms[1] + terms[2]

                if far:
                    @pl.when(jnp.logical_and(last, a == 2))
                    def _():
                        home_mid(g, 0).start()
                        home_mid(g, 1).start()
                for d in range(len(near)):
                    @pl.when(jnp.logical_and(last, a == near[d]))
                    def _():
                        home_near(g, d, 0).start()
                return c
            with jax.named_scope('combine'):
                lax.fori_loop(0, side, source, 0)

    def send_home(q, carry):
        backward(q)
        return carry

    def sum_up(q, carry):
        combine(q)
        return carry

    lax.fori_loop(0, chunks, send_home, 0)
    lax.fori_loop(0, chunks, sum_up, 0)
    own = pltpu.make_async_copy(parts.at[0], y_own, out_sem)
    own.start()
    for g in arrival:
        for d in range(len(near)):
            if far:
                with jax.named_scope('mid_wait'):
                    home_mid(g, d).wait_recv()
                parts[near[d], half(d), columns(g)] += mids[d, :, columns(g)]
            home_near(g, d, 1).start()

    for g in range(count):
        def drain(q, c):
            third_all(g, q, b1_sem, c1_sem).wait_send()
            home_second_all(g, q).wait_send()
            return c
        lax.fori_loop(0, chunks, drain, 0)
        for d in range(len(near)):
            gather_near(g, d, 0).wait_send()
            gather_near(g, d, 1).wait_send()
            if far:
                gather_far(g, d).wait_send()
                home_mid(g, d).wait_send()
    for o in range(3):
        gather_info_all(o).wait_send()
    for g in arrival:
        for d in range(len(near)):
            for i in range(2):
                with jax.named_scope('r3_wait'):
                    home_near(g, d, i).wait_recv()
                    home_near(g, d, i).wait_send()
    own.wait()


def solution(mesh):
    group_size = mesh.shape['ep']
    side = torus_side(group_size)
    row_spec = P(('dp', 'ep'), None)
    expert_spec = P('ep', None, None)

    def device_step(tokens, routes, w_router, w_one, w_three, w_two):
        num_tokens, d_model = tokens.shape
        top_k = routes.shape[1]
        num_experts = w_router.shape[1]
        d_expert = w_one.shape[2]
        capacity = slot_capacity(num_tokens, top_k, num_experts)
        chunks = capacity // SLOTS
        groups = column_groups(d_model)
        count = len(groups)
        plane = 2 * side * side
        hbm = pl.BlockSpec(memory_space=pl.ANY)
        vmem = pl.BlockSpec(memory_space=pltpu.VMEM)
        dma = pltpu.SemaphoreType.DMA
        slab = [[pltpu.VMEM((chunks, side, side, 2 * side, SLOTS, width), jnp.bfloat16) for _, width in groups] for _ in range(2)]
        pair = [dma((count, chunks)), dma((count, chunks))]
        y_own, y_peers = pl.pallas_call(
            functools.partial(moe_kernel, side, chunks, groups),
            out_shape=(jax.ShapeDtypeStruct((num_tokens, d_model), jnp.float32),
                       jax.ShapeDtypeStruct((2 if side > 2 else 1, num_tokens, d_model), jnp.float32)),
            in_specs=[hbm, vmem, hbm, hbm, hbm, hbm],
            out_specs=(hbm, hbm),
            scratch_shapes=[
                [pltpu.VMEM((side, num_tokens, width), jnp.bfloat16) for _, width in groups],
                pltpu.VMEM((3, side, 2 * top_k, num_tokens), jnp.float32),
                pltpu.VMEM((2 * top_k, num_tokens), jnp.float32),
                [pltpu.VMEM((side, 2 * plane, num_tokens), jnp.float32) for _ in ORDERS],
                slab[0], slab[1],
                pltpu.VMEM((chunks, side, side, side, 2, SLOTS, d_model), jnp.bfloat16),
                pltpu.VMEM((d_model, num_experts), jnp.bfloat16),
                pltpu.VMEM((d_model, d_expert), jnp.bfloat16),
                pltpu.VMEM((d_model, d_expert), jnp.bfloat16),
                pltpu.VMEM((d_expert, d_model), jnp.bfloat16),
                pltpu.VMEM((side, num_tokens, d_model), jnp.float32),
                pltpu.VMEM((2, num_tokens // 2, d_model), jnp.float32),
                dma((count + 1,)), dma((3,)), dma((count, 6)), dma((count, 6)), dma((3,)), dma((3,)),
                *pair, *pair, *pair, *pair, dma((count, 6)), dma((count, 6)), dma,
                pltpu.SemaphoreType.REGULAR((count, chunks)), pltpu.SemaphoreType.REGULAR((count, chunks)),
            ],
            compiler_params=pltpu.CompilerParams(collective_id=0, has_side_effects=True, vmem_limit_bytes=67043328),
            name='moe',
        )(tokens, routes.T, w_router, w_one[0], w_three[0], w_two[0])
        total = y_own
        for i in range(y_peers.shape[0]):
            total = total + y_peers[i]
        return total.astype(jnp.bfloat16)

    return jax.shard_map(device_step, mesh=mesh, in_specs=(row_spec, row_spec, P(None, None), expert_spec, expert_spec, expert_spec), out_specs=row_spec, check_vma=False)
```

profile of v0, /device:TPU:0, one launch (start us, length us, event | category | flops | bytes accessed | tf_op | source)
XLA Modules:
  0.0 234.8 jit_solution(7049423389561978810)
XLA Ops:
  0.0 230.5 %moe.1 = (f32[256,2048]{1,0:T(8,128)}, f32[2,256,2048]{2,1,0:T(8,128)}) custom-call(bf16[256,2048]{1,0:T(8,128)(2,1)} %tokens_hbm.1, s32[8,256]{1,0:T(8,128)} %bitcast.15, bf16[2048,128]{1,0:T(8,128)(2,1)} %w_router_hbm.1, bf16[2048,768]{1,0:T(8,128)(2,1)} %bitcast.12, bf16[2048,768]{1,0:T(8,128)(2,1)} %bitcast.13, bf16[768,2048]{1,0:T(8,128)(2,1)} %bitcast.14), custom_call_target="tpu_custom_call" | custom-call | tf_op jit(solution)/shard_map/moe/pallas_call | solution.py:437
  230.5 4.3 %fusion = bf16[256,2048]{1,0:T(8,128)(2,1)} fusion(f32[256,2048]{1,0:T(8,128)} %get-tuple-element.7, f32[2,256,2048]{2,1,0:T(8,128)} %get-tuple-element.8), kind=kLoop, calls=%fused_computation.1 | loop fusion | flops 1572864 | bytes 7340032 | tf_op jit(solution)/shard_map/convert_element_type | solution.py:466
where the time goes:
time: 235 us
  Pallas kernels  231 us (98%)
  other arithmetic  4.27 us (2%)
    pallas_call x1, Pallas kernels, device_step(): pl.pallas_call(functools.partial(moe_kernel, side, chunks, groups), out_s...  231 us

commit v1 on v0

--- a/solution.py
+++ b/solution.py
@@ -382,7 +382,7 @@
     lax.fori_loop(0, chunks, sum_up, 0)
     own = pltpu.make_async_copy(parts.at[0], y_own, out_sem)
     own.start()
-    for g in arrival:
+    for g in ((0, 1, 2, 3, 5, 4) if count == 6 else arrival):
         for d in range(len(near)):
             if far:
                 with jax.named_scope('mid_wait'):

time: 235 us -> 235 us (level)
  no operation moved by 1% of the time
where the time goes in v1:
time: 235 us
  Pallas kernels  231 us (98%)
  other arithmetic  4.27 us (2%)
    pallas_call x1, Pallas kernels, device_step(): pl.pallas_call(functools.partial(moe_kernel, side, chunks, groups), out_s...  231 us

profile of v1, /device:TPU:0, one launch (start us, length us, event | category | flops | bytes accessed | tf_op | source)
XLA Modules:
  0.0 234.8 jit_solution(10195601472066387143)
XLA Ops:
  0.0 230.5 %moe.1 = (f32[256,2048]{1,0:T(8,128)}, f32[2,256,2048]{2,1,0:T(8,128)}) custom-call(bf16[256,2048]{1,0:T(8,128)(2,1)} %tokens_hbm.1, s32[8,256]{1,0:T(8,128)} %bitcast.15, bf16[2048,128]{1,0:T(8,128)(2,1)} %w_router_hbm.1, bf16[2048,768]{1,0:T(8,128)(2,1)} %bitcast.12, bf16[2048,768]{1,0:T(8,128)(2,1)} %bitcast.13, bf16[768,2048]{1,0:T(8,128)(2,1)} %bitcast.14), custom_call_target="tpu_custom_call" | custom-call | tf_op jit(solution)/shard_map/moe/pallas_call | solution.py:437
  230.5 4.3 %fusion = bf16[256,2048]{1,0:T(8,128)(2,1)} fusion(f32[256,2048]{1,0:T(8,128)} %get-tuple-element.7, f32[2,256,2048]{2,1,0:T(8,128)} %get-tuple-element.8), kind=kLoop, calls=%fused_computation.1 | loop fusion | flops 1572864 | bytes 7340032 | tf_op jit(solution)/shard_map/convert_element_type | solution.py:466

commit v2 on v1

--- a/solution.py
+++ b/solution.py
@@ -217,7 +217,7 @@
         out = jnp.dot(select, toks[g][a], preferred_element_type=jnp.float32)
         out = out.reshape(side, ends, SLOTS, groups[g][1]).astype(jnp.bfloat16)
         packed[g][q, pl.ds(1, side - 1), a] = out[1:]
-        each(1, side, lambda b: out_second(g, q, a, b).start())
+        each(1, side, lambda b: out_second(g, q, a, b % (side - 1) + 1).start())
         relay_slab(g, q, a, 0)[...] = out[0]
 
     def pack_own(q, carry):
@@ -311,7 +311,7 @@
             with jax.named_scope('r1_wait'):
                 third_all(g, q, b1_sem, c1_sem).wait_recv()
             pl.semaphore_wait(free2_sem.at[g, q], side - 1)
-            each(1, side, lambda b: home_second(g, q, b).start())
+            each(1, side, lambda b: home_second(g, q, b % (side - 1) + 1).start())
             packed[g][q, 0] = relay_from(g, q, 0)[...]
 
     ahead = w_one.shape[1] >= 3 * packed_rows and w_one.shape[0] >= 2 * side * num_tokens

time: 235 us -> 235 us (level)
  no operation moved by 1% of the time
where the time goes in v2:
time: 235 us
  Pallas kernels  231 us (98%)
  other arithmetic  4.27 us (2%)
    pallas_call x1, Pallas kernels, device_step(): pl.pallas_call(functools.partial(moe_kernel, side, chunks, groups), out_s...  231 us

profile of v2, /device:TPU:0, one launch (start us, length us, event | category | flops | bytes accessed | tf_op | source)
XLA Modules:
  0.0 234.8 jit_solution(9896706473288458167)
XLA Ops:
  0.0 230.5 %moe.1 = (f32[256,2048]{1,0:T(8,128)}, f32[2,256,2048]{2,1,0:T(8,128)}) custom-call(bf16[256,2048]{1,0:T(8,128)(2,1)} %tokens_hbm.1, s32[8,256]{1,0:T(8,128)} %bitcast.15, bf16[2048,128]{1,0:T(8,128)(2,1)} %w_router_hbm.1, bf16[2048,768]{1,0:T(8,128)(2,1)} %bitcast.12, bf16[2048,768]{1,0:T(8,128)(2,1)} %bitcast.13, bf16[768,2048]{1,0:T(8,128)(2,1)} %bitcast.14), custom_call_target="tpu_custom_call" | custom-call | tf_op jit(solution)/shard_map/moe/pallas_call | solution.py:437
  230.5 4.3 %fusion = bf16[256,2048]{1,0:T(8,128)(2,1)} fusion(f32[256,2048]{1,0:T(8,128)} %get-tuple-element.7, f32[2,256,2048]{2,1,0:T(8,128)} %get-tuple-element.8), kind=kLoop, calls=%fused_computation.1 | loop fusion | flops 1572864 | bytes 7340032 | tf_op jit(solution)/shard_map/convert_element_type | solution.py:466
